TPU v7x, 64 devices: a 2x2x8 block of a 4x4x8 slice. The times are simulated.
64 devices in a mesh: dp: 4 (over x, y), sp: 16 (over z, core).
Axes of the slice: x: 2, y: 2, z: 8, core: 2. Of those that a mesh axis runs over, the one named last changes fastest.
The devices are a block of a 4x4x8 slice.
Arguments:
- q: bfloat16 [128, 16, 256], P('dp'), parts along dimension 0
- k: bfloat16 [128, 4096, 8, 256], P('dp', 'sp'), parts along dimension 0
- v: bfloat16 [128, 4096, 8, 256], P('dp', 'sp'), parts along dimension 0
Outputs:
- q: bfloat16 [128, 16, 256], P('dp'), parts along dimension 0
There are 4 independent parts. A program takes and returns all parts, laid end to end along the dimension named above; each array names one.
All inputs are finite; a program needn't handle non-finite values.
Results may differ from a plain program's by a relative error of at most 0.012.
Values are sent between devices in bfloat16 or wider.
A program may use at most 768 MiB of HBM per device.

v0:
```python
import jax
import jax.numpy as jnp
from jax import lax
from jax.sharding import PartitionSpec as P


def einsum(form, a, b):
    return jnp.einsum(form, a.astype(jnp.float32), b.astype(jnp.float32))


def part_of(q, k, v):
    grouped = q.reshape(q.shape[0], k.shape[2], -1, q.shape[2])
    scores = einsum("bgsd,bugd->bgsu", grouped, k) * q.shape[2] ** -0.5
    high = jnp.max(scores, -1, keepdims=True)
    weights = jnp.exp(scores - high)
    seen = einsum("bgsu,bugd->bgsd", weights.astype(jnp.bfloat16), v)
    return jnp.concatenate([seen, jnp.sum(weights, -1, keepdims=True), high], -1)


def together(parts):
    seen, total, high = parts[..., :-2], parts[..., -2:-1], parts[..., -1:]
    scale = jnp.exp(high - jnp.max(high, 0))
    return (jnp.sum(seen * scale, 0) / jnp.sum(total * scale, 0)).astype(jnp.bfloat16)


def solution(mesh):
    def step(q, k, v):
        return together(lax.all_gather(part_of(q, k, v), "sp")).reshape(q.shape)

    return jax.shard_map(
        step,
        mesh=mesh,
        in_specs=(P("dp", None, None), P("dp", "sp", None, None), P("dp", "sp", None, None)),
        out_specs=P("dp", None, None),
        check_vma=False,
    )
```

profile of v0, /device:TPU:21, one launch (start us, length us, event | category | flops | bytes accessed | tf_op | source)
XLA Modules:
  0.0 155.8 jit_solution(1488381013536087285)
XLA Ops:
  6.5 0.0 all-gather.3.cloned.1.call-start
  6.6 1.1 reshape.15
  7.6 18.3 %fusion.15 = (f32[32,8,2]{2,1,0:T(8,128)S(1)}, f32[32,8,2,256]{3,2,1,0:T(2,128)S(1)}) fusion(bf16[32,8,2,256]{3,2,1,0:T(2,128)(2,1)S(1)} %reshape.15, bf16[32,256,8,256]{3,2,1,0:T(8,128)(2,1)} %param.4), kind=kOutput, calls=%fused_computation.19 | convolution fusion | flops 67370496 | bytes 34342912 | tf_op jit(solution)/shard_map/bgsd,bugd->bgsu/dot_general | solution.py:8
  25.9 0.7 fusion.9
  26.7 19.1 %fusion = f32[32,8,2,256]{3,2,1,0:T(2,128)S(1)} fusion(bf16[32,256,8,256]{3,2,1,0:T(8,128)(2,1)} %param.5, f32[32,8,2,256]{3,2,1,0:T(2,128)S(1)} %get-tuple-element.11, f32[32,8,2]{2,1,0:T(8,128)S(1)} %get-tuple-element.10), kind=kOutput, calls=%fused_computation | convolution fusion | flops 67371008 | bytes 34605056 | tf_op jit(solution)/shard_map/bgsu,bugd->bgsd/dot_general | solution.py:8
  45.8 1.7 %copy.65 = f32[32,8,2,1]{3,2,1,0:T(2,128)S(1)} copy(f32[32,8,2,1]{2,1,0,3:T(8,128)S(1)} %bitcast.14) | data formatting | bytes 4096 | tf_op jit(solution)/shard_map/broadcast_in_dim | solution.py:17
  47.5 1.7 %copy.66 = f32[32,8,2,1]{3,2,1,0:T(2,128)S(1)} copy(f32[32,8,2,1]{2,1,0,3:T(8,128)S(1)} %bitcast.13) | data formatting | bytes 4096 | tf_op jit(solution)/shard_map/broadcast_in_dim | solution.py:14
  49.1 0.5 pad_maximum_fusion
  49.7 1.0 copy.67
  50.7 0.1 all-gather.3.cloned.1.call-update
  50.7 77.4 %all-gather.3.cloned.1.call-done = f32[512,8,2,258]{3,1,2,0:T(8,128)} async-done(((f32[32,8,2,258]{3,1,2,0:T(8,128)}), f32[512,8,2,258]{3,1,2,0:T(8,128)}) %all-gather.3.cloned.1.call-update) | async-done | bytes 8454160 | tf_op jit(solution)/shard_map/all_gather | solution.py:28
  128.1 8.4 %fusion.14 = (f32[16,32,8,2,1]{4,2,3,1,0:T(8,128)}, f32[32,8,2]{1,2,0:T(2,128)S(1)}, f32[16,32,8,2,1]{4,2,3,1,0:T(8,128)}) fusion(f32[16,32,8,2,258]{4,2,3,1,0:T(8,128)} %bitcast.11), kind=kLoop, calls=%fused_computation.18 | loop fusion | flops 7680 | bytes 133120 | tf_op jit(solution)/shard_map/slice | solution.py:21
  136.5 3.3 %copy.79 = f32[16,32,8,2,1]{1,2,4,3,0:T(8,128)S(1)} copy(f32[16,32,8,2,1]{4,2,3,1,0:T(8,128)} %get-tuple-element.5) | data formatting | bytes 65536
  139.8 0.1 copy.80
  139.8 3.3 %copy.78 = f32[16,32,8,2,1]{1,2,4,3,0:T(8,128)S(1)} copy(f32[16,32,8,2,1]{4,2,3,1,0:T(8,128)} %get-tuple-element.7) | data formatting | bytes 65536
  143.2 0.3 copy.69
  143.4 4.2 %fusion.4 = f32[32,8,2,256]{3,1,2,0:T(8,128)S(1)} fusion(f32[16,32,8,2,258]{4,2,3,1,0:T(8,128)} %bitcast.12, f32[16,32,8,2]{2,3,1,0:T(2,128)S(1)} %copy.69), kind=kLoop, calls=%fused_computation.5 | loop fusion | flops 4063232 | bytes 8945664 | tf_op jit(solution)/shard_map/reduce_sum | solution.py:23
  147.6 0.3 copy.70
  147.9 0.1 fusion.8
  148.1 0.9 copy.73
  (2 shorter events, 0.0 us)
Async XLA Ops:
  6.5 121.6 %all-gather.3.cloned.1.call-start = ((), (), s32[]{:S(2)}) async-start(), calls=%async_computation | async-start | bytes 13369344 | tf_op jit(solution)/shard_map/all_gather | solution.py:28
Sparse Core Ops, SparseCore 0:
  50.8 77.2 all-gather.2
where the time goes:
time: 156 us
  waiting for transfers between devices  77.5 us (50%)
  matrix products  37.5 us (24%)
  other arithmetic  14 us (9%)
  between operations  13.5 us (9%)
  local copies, waits for them, and re-layouts  13.4 us (9%)
    all_gather x1, waiting for transfers between devices, step(): return together(lax.all_gather(part_of(q, k, v), 'sp')).reshape(q.shape)  77.4 us
    dot_general x2, matrix products, einsum(): return jnp.einsum(form, a.astype(jnp.float32), b.astype(jnp.float32))  37.5 us
    slice x1, other arithmetic, together(): seen, total, high = (parts[..., :-2], parts[..., -2:-1], parts[..., -1:])  8.36 us
    unnamed x3, local copies, waits for them, and re-layouts  6.59 us
    reduce_sum x1, other arithmetic, together(): jnp.sum(seen * scale, 0) / jnp.sum(total * scale, 0)  4.17 us
  transfers between devices with their start and end apart: 1, of which 1 were waited for; matrix products, arithmetic and copies ran while one was open for 0% of the time, Pallas kernels for 0%

commit v1 on v0

v1 whole, which is shorter than its diff:
```python
import functools

import jax
import jax.numpy as jnp
from jax import lax
from jax.experimental import pallas as pl
from jax.experimental.pallas import tpu as pltpu
from jax.sharding import PartitionSpec as P

MESH = pl.DeviceIdType.MESH
SLOTS = 6
LAG = 10
STRIDE = 5
BACK = 13


def kernel(n, p, rows, heads, head, kv, q_ref, k_hbm, v_hbm, out_ref, kbuf, vbuf, scores, weights, mine, stat, parts, stats,
           ksem, vsem, part_send, part_recv, stat_send, stat_recv, out_send, out_recv):
    me = lax.axis_index("sp")
    group = heads // kv
    scale = head ** -0.5

    def other(d):
        return lax.rem(me + d, p)

    def fetch_k(s, slot):
        return pltpu.make_async_copy(k_hbm.at[s], kbuf.at[slot], ksem.at[slot])

    def fetch_v(s, slot):
        return pltpu.make_async_copy(v_hbm.at[s], vbuf.at[slot], vsem.at[slot])

    for s in range(SLOTS):
        fetch_k(s, s).start()
        fetch_v(s, s).start()

    barrier = pltpu.get_barrier_semaphore()
    for d in range(1, p):
        pl.semaphore_signal(barrier, inc=1, device_id={"sp": other(d)}, device_id_type=MESH)

    row = lax.broadcasted_iota(jnp.int32, (heads, rows), 0)
    col = lax.broadcasted_iota(jnp.int32, (heads, rows), 1)
    own = (col % kv) == (row // group)
    half = heads // 2
    row1 = lax.broadcasted_iota(jnp.int32, (heads, 128), 0)
    col1 = lax.broadcasted_iota(jnp.int32, (heads, 128), 1)
    at_high, at_total = col1 == row1, col1 == row1 + 64

    def owner(s):
        return lax.rem(s * STRIDE, p)

    def score(s, slot):
        scores[...] = lax.dot_general(q_ref[s], kbuf[slot], (((1,), (1,)), ((), ())), preferred_element_type=jnp.float32)

    def soften(s):
        x = jnp.where(own, scores[...], -jnp.inf)
        high = jnp.max(x, axis=1, keepdims=True)
        w = jnp.exp((x - high) * scale)
        weights[...] = w.astype(jnp.bfloat16)
        total = jnp.sum(w, axis=1, keepdims=True)
        spread = jnp.where(at_high, high * scale, jnp.where(at_total, total, 0.0))
        stat[s] = spread[:half] + spread[half:]

    def mix(s, slot):
        mine[s] = jnp.dot(weights[...], vbuf[slot], preferred_element_type=jnp.float32).astype(jnp.bfloat16)

    def to_owner(s, src, dst, send, recv):
        who = owner(s)
        turn = s // p
        place = lax.rem(me - who - 1 + 2 * p, p)

        @pl.when(who != me)
        def _():
            pltpu.make_async_remote_copy(
                src_ref=src.at[s], dst_ref=dst.at[turn, place], send_sem=send, recv_sem=recv.at[turn], device_id={"sp": who}, device_id_type=MESH
            ).start()

    def send_stat(s):
        to_owner(s, stat, stats, stat_send, stat_recv)

    def send_part(s):
        to_owner(s, mine, parts, part_send, part_recv)

    def all_of(ref, sem):
        return pltpu.make_async_copy(ref, ref, sem)

    def together(s):
        turn = s // p
        all_of(stats.at[turn], stat_recv.at[turn]).wait()
        high, total = [], []
        for j in range(p):
            x = stat[s] if j == p - 1 else stats[turn, j]
            x = jnp.concatenate([x, x], axis=0)
            high.append(jnp.sum(jnp.where(at_high, x, 0.0), axis=1, keepdims=True))
            total.append(jnp.sum(jnp.where(at_total, x, 0.0), axis=1, keepdims=True))
        top = functools.reduce(jnp.maximum, high)
        share = [jnp.exp(h - top) for h in high]
        whole = functools.reduce(jnp.add, [a * t for a, t in zip(share, total)])
        all_of(parts.at[turn], part_recv.at[turn]).wait()
        seen = jnp.zeros((heads, head), jnp.float32)
        for j in range(p):
            x = mine[s] if j == p - 1 else parts[turn, j]
            seen = seen + x.astype(jnp.float32) * share[j]
        out_ref[s] = (seen / whole).astype(out_ref.dtype)
        for d in range(1, p):
            pltpu.make_async_remote_copy(
                src_ref=out_ref.at[s], dst_ref=out_ref.at[s], send_sem=out_send, recv_sem=out_recv, device_id={"sp": other(d)}, device_id_type=MESH
            ).start()

    fetch_k(0, 0).wait()
    score(0, 0)
    fetch_k(1, 1).wait()
    soften(0)
    score(1, 1)
    for s in (0, 1):
        fetch_k(s + SLOTS, s).start()
    pl.semaphore_wait(barrier, p - 1)
    send_stat(0)

    def body(s, _):
        kslot, vslot = lax.rem(s, SLOTS), lax.rem(s - 2, SLOTS)
        fetch_v(s - 2, vslot).wait()
        fetch_k(s, kslot).wait()
        mix(s - 2, vslot)
        soften(s - 1)
        score(s, kslot)

        @pl.when(s + SLOTS < n)
        def _():
            fetch_k(s + SLOTS, kslot).start()

        @pl.when(s - 2 + SLOTS < n)
        def _():
            fetch_v(s - 2 + SLOTS, vslot).start()

        send_stat(s - 1)
        send_part(s - 2)

        @pl.when((s >= LAG) & (owner(jnp.maximum(s - LAG, 0)) == me))
        def _():
            together(s - LAG)

        return 0

    lax.fori_loop(2, n, body, 0)
    slot = (n - 2) % SLOTS
    fetch_v(n - 2, slot).wait()
    mix(n - 2, slot)
    soften(n - 1)
    send_stat(n - 1)
    send_part(n - 2)
    slot = (n - 1) % SLOTS
    fetch_v(n - 1, slot).wait()
    mix(n - 1, slot)
    send_part(n - 1)
    last = n - p + lax.rem(me * BACK, p)

    @pl.when(last >= n - LAG)
    def _():
        together(last)

    turns = n // p
    all_of(out_ref.at[pl.ds(0, n - turns)], out_recv).wait()
    all_of(mine.at[pl.ds(0, n - turns)], part_send).wait()
    all_of(stat.at[pl.ds(0, n - turns)], stat_send).wait()
    all_of(out_ref.at[pl.ds(0, turns * (p - 1))], out_send).wait()


def solution(mesh):
    p = mesh.shape["sp"]

    def step(q, k, v):
        n, heads, head = q.shape
        tokens, kv = k.shape[1:3]
        rows = tokens * kv
        turns = n // p
        assert turns * p == n and (STRIDE * BACK) % p == 1
        return pl.pallas_call(
            functools.partial(kernel, n, p, rows, heads, head, kv),
            out_shape=jax.ShapeDtypeStruct(q.shape, q.dtype),
            in_specs=[pl.BlockSpec(memory_space=pltpu.VMEM), pl.BlockSpec(memory_space=pl.ANY), pl.BlockSpec(memory_space=pl.ANY)],
            out_specs=pl.BlockSpec(memory_space=pltpu.VMEM),
            scratch_shapes=[
                pltpu.VMEM((SLOTS, rows, head), jnp.bfloat16),
                pltpu.VMEM((SLOTS, rows, head), jnp.bfloat16),
                pltpu.VMEM((heads, rows), jnp.float32),
                pltpu.VMEM((heads, rows), jnp.bfloat16),
                pltpu.VMEM((n, heads, head), jnp.bfloat16),
                pltpu.VMEM((n, heads // 2, 128), jnp.float32),
                pltpu.VMEM((turns, p - 1, heads, head), jnp.bfloat16),
                pltpu.VMEM((turns, p - 1, heads // 2, 128), jnp.float32),
                pltpu.SemaphoreType.DMA((SLOTS,)),
                pltpu.SemaphoreType.DMA((SLOTS,)),
                pltpu.SemaphoreType.DMA,
                pltpu.SemaphoreType.DMA((turns,)),
                pltpu.SemaphoreType.DMA,
                pltpu.SemaphoreType.DMA((turns,)),
                pltpu.SemaphoreType.DMA,
                pltpu.SemaphoreType.DMA,
            ],
            compiler_params=pltpu.CompilerParams(vmem_limit_bytes=48 * 2**20, collective_id=0, has_side_effects=True),
            name="attend",
        )(q, k.reshape(n, rows, head), v.reshape(n, rows, head))

    return jax.shard_map(
        step,
        mesh=mesh,
        in_specs=(P("dp", None, None), P("dp", "sp", None, None), P("dp", "sp", None, None)),
        out_specs=P("dp", None, None),
        check_vma=False,
    )
```

time: 156 us -> 38.6 us (0.25)
  waiting for transfers between devices: 77.5 us -> 0 us
  matrix products: 37.5 us -> 0 us
  Pallas kernels: 0 us -> 36.9 us
  other arithmetic: 14 us -> 0 us
  between operations: 13.5 us -> 0.01 us
  local copies, waits for them, and re-layouts: 13.4 us -> 1.65 us
    all_gather x1 -> x0, waiting for transfers between devices: 77.4 us -> none  [step(): return together(lax.all_gather(part_of(q, k, v), 'sp')).reshape(q.shape)]
    dot_general x2 -> x0, matrix products: 37.5 us -> none  [einsum(): return jnp.einsum(form, a.astype(jnp.float32), b.astype(jnp.float32))]
    pallas_call x0 -> x1, Pallas kernels: none -> 36.9 us  [step(): pl.pallas_call(functools.partial(kernel, n, p, rows, heads, head, kv), ou...]
    slice x1 -> x0, other arithmetic: 8.36 us -> none  [together(): seen, total, high = (parts[..., :-2], parts[..., -2:-1], parts[..., -1:])]
    reduce_sum x3 -> x0, other arithmetic: 4.94 us -> none  [the longest x1 4.17 us: together(): jnp.sum(seen * scale, 0) / jnp.sum(total * scale, 0)]
    unnamed x3, local copies, waits for them, and re-layouts: 6.59 us -> 1.65 us
    broadcast_in_dim x2 -> x0, local copies, waits for them, and re-layouts: 3.33 us -> none  [the longest x1 1.66 us: part_of(): jnp.sum(weights, -1, keepdims=True)]
  transfers between devices with their start and end apart: 1 -> 0, of which waited for: 1 -> 0; matrix products, arithmetic and copies ran while one was open for 0% -> 0% of each run, Pallas kernels for 0% -> 0%
where the time goes in v1:
time: 38.6 us; the launch traced here: 38.5 us
  Pallas kernels  36.9 us (96%)
  local copies, waits for them, and re-layouts  1.65 us (4%)
    pallas_call x1, Pallas kernels, step(): pl.pallas_call(functools.partial(kernel, n, p, rows, heads, head, kv), ou...  36.9 us
    unnamed x3, local copies, waits for them, and re-layouts  1.65 us

profile of v1, /device:TPU:21, one launch (start us, length us, event | category | flops | bytes accessed | tf_op | source)
XLA Modules:
  0.0 38.5 jit_solution(16602156466530067217)
XLA Ops:
  0.0 0.0 copy-start
  0.0 0.9 %copy-done = bf16[32,16,256]{2,1,0:T(8,128)(2,1)S(1)} copy-done((bf16[32,16,256]{2,1,0:T(8,128)(2,1)S(1)}, bf16[32,16,256]{2,1,0:T(8,128)(2,1)}, u32[]{:S(2)}) %copy-start) | copy-done | bytes 262168
  1.0 36.9 %attend.1 = bf16[32,16,256]{2,1,0:T(8,128)(2,1)S(1)} custom-call(bf16[32,16,256]{2,1,0:T(8,128)(2,1)S(1)} %copy-done, bf16[32,2048,256]{2,1,0:T(8,128)(2,1)} %bitcast.2, bf16[32,2048,256]{2,1,0:T(8,128)(2,1)} %bitcast.3), custom_call_target="tpu_custom_call" | custom-call | tf_op jit(solution)/shard_map/attend/pallas_call | solution.py:177
  37.8 0.7 %copy.5 = bf16[32,16,256]{2,1,0:T(8,128)(2,1)} copy(bf16[32,16,256]{2,1,0:T(8,128)(2,1)S(1)} %attend.1) | data formatting | bytes 524288
Async XLA Ops:
  0.0 0.9 %copy-start = (bf16[32,16,256]{2,1,0:T(8,128)(2,1)S(1)}, bf16[32,16,256]{2,1,0:T(8,128)(2,1)}, u32[]{:S(2)}) copy-start(bf16[32,16,256]{2,1,0:T(8,128)(2,1)} %q_ref.1) | copy-start | bytes 786436

commit v2 on v1

--- a/solution.py
+++ b/solution.py
@@ -9,13 +9,14 @@
 
 MESH = pl.DeviceIdType.MESH
 SLOTS = 6
-LAG = 10
-STRIDE = 5
-BACK = 13
-
-
-def kernel(n, p, rows, heads, head, kv, q_ref, k_hbm, v_hbm, out_ref, kbuf, vbuf, scores, weights, mine, stat, parts, stats,
-           ksem, vsem, part_send, part_recv, stat_send, stat_recv, out_send, out_recv):
+OPEN = 8
+FIRST = 24
+LAG = 16
+ORDER = (4, 10, 6, 12, 8, 14, 2, 11, 5, 9, 3, 13, 7, 0, 15, 1)
+
+
+def kernel(n, p, rows, heads, head, kv, q_hbm, k_hbm, v_hbm, out_ref, q_ref, kbuf, vbuf, scores, weights, mine, stat, parts, stats,
+           qsem, ksem, vsem, part_send, part_recv, stat_send, stat_recv, out_send, out_recv):
     me = lax.axis_index("sp")
     group = heads // kv
     scale = head ** -0.5
@@ -29,9 +30,11 @@
     def fetch_v(s, slot):
         return pltpu.make_async_copy(v_hbm.at[s], vbuf.at[slot], vsem.at[slot])
 
+    fetch_q = pltpu.make_async_copy(q_hbm, q_ref, qsem)
+    fetch_q.start()
     for s in range(SLOTS):
-        fetch_k(s, s).start()
-        fetch_v(s, s).start()
+        fetch_k(s, s).start(priority=1)
+        fetch_v(s, s).start(priority=1)
 
     barrier = pltpu.get_barrier_semaphore()
     for d in range(1, p):
@@ -40,13 +43,16 @@
     row = lax.broadcasted_iota(jnp.int32, (heads, rows), 0)
     col = lax.broadcasted_iota(jnp.int32, (heads, rows), 1)
     own = (col % kv) == (row // group)
-    half = heads // 2
     row1 = lax.broadcasted_iota(jnp.int32, (heads, 128), 0)
     col1 = lax.broadcasted_iota(jnp.int32, (heads, 128), 1)
     at_high, at_total = col1 == row1, col1 == row1 + 64
 
     def owner(s):
-        return lax.rem(s * STRIDE, p)
+        j = lax.rem(s, p)
+        return functools.reduce(jnp.add, [jnp.where(j == i, d, 0) for i, d in enumerate(ORDER)])
+
+    def owned(turn):
+        return turn * p + functools.reduce(jnp.add, [jnp.where(me == d, i, 0) for i, d in enumerate(ORDER)])
 
     def score(s, slot):
         scores[...] = lax.dot_general(q_ref[s], kbuf[slot], (((1,), (1,)), ((), ())), preferred_element_type=jnp.float32)
@@ -58,7 +64,7 @@
         weights[...] = w.astype(jnp.bfloat16)
         total = jnp.sum(w, axis=1, keepdims=True)
         spread = jnp.where(at_high, high * scale, jnp.where(at_total, total, 0.0))
-        stat[s] = spread[:half] + spread[half:]
+        stat[s] = jnp.sum(spread, axis=0, keepdims=True)
 
     def mix(s, slot):
         mine[s] = jnp.dot(weights[...], vbuf[slot], preferred_element_type=jnp.float32).astype(jnp.bfloat16)
@@ -89,7 +95,6 @@
         high, total = [], []
         for j in range(p):
             x = stat[s] if j == p - 1 else stats[turn, j]
-            x = jnp.concatenate([x, x], axis=0)
             high.append(jnp.sum(jnp.where(at_high, x, 0.0), axis=1, keepdims=True))
             total.append(jnp.sum(jnp.where(at_total, x, 0.0), axis=1, keepdims=True))
         top = functools.reduce(jnp.maximum, high)
@@ -106,15 +111,14 @@
                 src_ref=out_ref.at[s], dst_ref=out_ref.at[s], send_sem=out_send, recv_sem=out_recv, device_id={"sp": other(d)}, device_id_type=MESH
             ).start()
 
+    fetch_q.wait()
     fetch_k(0, 0).wait()
     score(0, 0)
     fetch_k(1, 1).wait()
     soften(0)
     score(1, 1)
     for s in (0, 1):
-        fetch_k(s + SLOTS, s).start()
-    pl.semaphore_wait(barrier, p - 1)
-    send_stat(0)
+        fetch_k(s + SLOTS, s).start(priority=1)
 
     def body(s, _):
         kslot, vslot = lax.rem(s, SLOTS), lax.rem(s - 2, SLOTS)
@@ -126,16 +130,34 @@
 
         @pl.when(s + SLOTS < n)
         def _():
-            fetch_k(s + SLOTS, kslot).start()
+            fetch_k(s + SLOTS, kslot).start(priority=1)
 
         @pl.when(s - 2 + SLOTS < n)
         def _():
-            fetch_v(s - 2 + SLOTS, vslot).start()
-
-        send_stat(s - 1)
-        send_part(s - 2)
-
-        @pl.when((s >= LAG) & (owner(jnp.maximum(s - LAG, 0)) == me))
+            fetch_v(s - 2 + SLOTS, vslot).start(priority=1)
+
+        @pl.when(s == OPEN)
+        def _():
+            pl.semaphore_wait(barrier, p - 1)
+
+            def late(u, _):
+                send_stat(u)
+                send_part(u)
+                return 0
+
+            lax.fori_loop(0, OPEN - 2, late, 0)
+            send_stat(OPEN - 2)
+
+        @pl.when(s >= OPEN)
+        def _():
+            send_stat(s - 1)
+            send_part(s - 2)
+
+        @pl.when(s == FIRST)
+        def _():
+            together(owned(0))
+
+        @pl.when((s >= p + LAG) & (owner(jnp.maximum(s - LAG, 0)) == me))
         def _():
             together(s - LAG)
 
@@ -152,11 +174,9 @@
     fetch_v(n - 1, slot).wait()
     mix(n - 1, slot)
     send_part(n - 1)
-    last = n - p + lax.rem(me * BACK, p)
-
-    @pl.when(last >= n - LAG)
+    @pl.when(owned(1) >= n - LAG)
     def _():
-        together(last)
+        together(owned(1))
 
     turns = n // p
     all_of(out_ref.at[pl.ds(0, n - turns)], out_recv).wait()
@@ -173,21 +193,23 @@
         tokens, kv = k.shape[1:3]
         rows = tokens * kv
         turns = n // p
-        assert turns * p == n and (STRIDE * BACK) % p == 1
+        assert n == 2 * p and sorted(ORDER) == list(range(p)) and FIRST >= p + 2
         return pl.pallas_call(
             functools.partial(kernel, n, p, rows, heads, head, kv),
             out_shape=jax.ShapeDtypeStruct(q.shape, q.dtype),
-            in_specs=[pl.BlockSpec(memory_space=pltpu.VMEM), pl.BlockSpec(memory_space=pl.ANY), pl.BlockSpec(memory_space=pl.ANY)],
+            in_specs=[pl.BlockSpec(memory_space=pltpu.HBM)] * 3,
             out_specs=pl.BlockSpec(memory_space=pltpu.VMEM),
             scratch_shapes=[
+                pltpu.VMEM((n, heads, head), jnp.bfloat16),
                 pltpu.VMEM((SLOTS, rows, head), jnp.bfloat16),
                 pltpu.VMEM((SLOTS, rows, head), jnp.bfloat16),
                 pltpu.VMEM((heads, rows), jnp.float32),
                 pltpu.VMEM((heads, rows), jnp.bfloat16),
                 pltpu.VMEM((n, heads, head), jnp.bfloat16),
-                pltpu.VMEM((n, heads // 2, 128), jnp.float32),
+                pltpu.VMEM((n, 1, 128), jnp.float32),
                 pltpu.VMEM((turns, p - 1, heads, head), jnp.bfloat16),
-                pltpu.VMEM((turns, p - 1, heads // 2, 128), jnp.float32),
+                pltpu.VMEM((turns, p - 1, 1, 128), jnp.float32),
+                pltpu.SemaphoreType.DMA,
                 pltpu.SemaphoreType.DMA((SLOTS,)),
                 pltpu.SemaphoreType.DMA((SLOTS,)),
                 pltpu.SemaphoreType.DMA,
@@ -199,7 +221,7 @@
             ],
             compiler_params=pltpu.CompilerParams(vmem_limit_bytes=48 * 2**20, collective_id=0, has_side_effects=True),
             name="attend",
-        )(q, k.reshape(n, rows, head), v.reshape(n, rows, head))
+        )(pltpu.with_memory_space_constraint(q, pltpu.HBM), k.reshape(n, rows, head), v.reshape(n, rows, head))
 
     return jax.shard_map(
         step,

time: 38.6 us -> 36.1 us (0.935)
  Pallas kernels: 36.9 us -> 35.3 us
  local copies, waits for them, and re-layouts: 1.65 us -> 0.71 us
    pallas_call x1, Pallas kernels: 36.9 us -> 35.3 us  [step(): pl.pallas_call(functools.partial(kernel, n, p, rows, heads, head, kv), ou...]
    unnamed x3 -> x1, local copies, waits for them, and re-layouts: 1.65 us -> 0.71 us
where the time goes in v2:
time: 36.1 us
  Pallas kernels  35.3 us (98%)
  local copies, waits for them, and re-layouts  0.71 us (2%)
    pallas_call x1, Pallas kernels, step(): pl.pallas_call(functools.partial(kernel, n, p, rows, heads, head, kv), ou...  35.3 us

profile of v2, /device:TPU:21, one launch (start us, length us, event | category | flops | bytes accessed | tf_op | source)
XLA Modules:
  0.0 36.1 jit_solution(14734508411369646460)
XLA Ops:
  0.0 35.3 %attend.1 = bf16[32,16,256]{2,1,0:T(8,128)(2,1)S(1)} custom-call(bf16[32,16,256]{2,1,0:T(8,128)(2,1)} %q_hbm.1, bf16[32,2048,256]{2,1,0:T(8,128)(2,1)} %bitcast.2, bf16[32,2048,256]{2,1,0:T(8,128)(2,1)} %bitcast.3), custom_call_target="tpu_custom_call" | custom-call | tf_op jit(solution)/shard_map/attend/pallas_call | solution.py:197
  35.4 0.7 %copy.5 = bf16[32,16,256]{2,1,0:T(8,128)(2,1)} copy(bf16[32,16,256]{2,1,0:T(8,128)(2,1)S(1)} %attend.1) | data formatting | bytes 524288

commit v3 on v2

--- a/solution.py
+++ b/solution.py
@@ -12,7 +12,7 @@
 OPEN = 8
 FIRST = 24
 LAG = 16
-ORDER = (4, 10, 6, 12, 8, 14, 2, 11, 5, 9, 3, 13, 7, 0, 15, 1)
+ORDER = (4, 10, 6, 12, 8, 14, 2, 11, 7, 9, 3, 13, 5, 0, 15, 1)
 
 
 def kernel(n, p, rows, heads, head, kv, q_hbm, k_hbm, v_hbm, out_ref, q_ref, kbuf, vbuf, scores, weights, mine, stat, parts, stats,
@@ -66,11 +66,12 @@
         spread = jnp.where(at_high, high * scale, jnp.where(at_total, total, 0.0))
         stat[s] = jnp.sum(spread, axis=0, keepdims=True)
 
-    def mix(s, slot):
-        mine[s] = jnp.dot(weights[...], vbuf[slot], preferred_element_type=jnp.float32).astype(jnp.bfloat16)
-
-    def to_owner(s, src, dst, send, recv):
-        who = owner(s)
+    def mix(s, slot, pieces=1):
+        step = rows // pieces
+        got = [jnp.dot(weights[:, i:i + step], vbuf[slot, i:i + step], preferred_element_type=jnp.float32) for i in range(0, rows, step)]
+        mine[s] = functools.reduce(jnp.add, got).astype(jnp.bfloat16)
+
+    def to_owner(s, who, src, dst, send, recv):
         turn = s // p
         place = lax.rem(me - who - 1 + 2 * p, p)
 
@@ -80,11 +81,11 @@
                 src_ref=src.at[s], dst_ref=dst.at[turn, place], send_sem=send, recv_sem=recv.at[turn], device_id={"sp": who}, device_id_type=MESH
             ).start()
 
-    def send_stat(s):
-        to_owner(s, stat, stats, stat_send, stat_recv)
-
-    def send_part(s):
-        to_owner(s, mine, parts, part_send, part_recv)
+    def send_stat(s, who):
+        to_owner(s, who, stat, stats, stat_send, stat_recv)
+
+    def send_part(s, who):
+        to_owner(s, who, mine, parts, part_send, part_recv)
 
     def all_of(ref, sem):
         return pltpu.make_async_copy(ref, ref, sem)
@@ -92,21 +93,18 @@
     def together(s):
         turn = s // p
         all_of(stats.at[turn], stat_recv.at[turn]).wait()
-        high, total = [], []
-        for j in range(p):
-            x = stat[s] if j == p - 1 else stats[turn, j]
-            high.append(jnp.sum(jnp.where(at_high, x, 0.0), axis=1, keepdims=True))
-            total.append(jnp.sum(jnp.where(at_total, x, 0.0), axis=1, keepdims=True))
-        top = functools.reduce(jnp.maximum, high)
-        share = [jnp.exp(h - top) for h in high]
-        whole = functools.reduce(jnp.add, [a * t for a, t in zip(share, total)])
+        rows = [stat[s] if j == p - 1 else stats[turn, j] for j in range(p)]
+        top = functools.reduce(jnp.maximum, rows)
+        share = [jnp.exp(x - top) for x in rows]
+        whole = functools.reduce(jnp.add, [a * pltpu.roll(x, 64, 1) for a, x in zip(share, rows)])
+        share = [jnp.sum(jnp.where(at_high, a / whole, 0.0), axis=1, keepdims=True) for a in share]
         all_of(parts.at[turn], part_recv.at[turn]).wait()
         seen = jnp.zeros((heads, head), jnp.float32)
         for j in range(p):
             x = mine[s] if j == p - 1 else parts[turn, j]
             seen = seen + x.astype(jnp.float32) * share[j]
-        out_ref[s] = (seen / whole).astype(out_ref.dtype)
-        for d in range(1, p):
+        out_ref[s] = seen.astype(out_ref.dtype)
+        for d in sorted(range(1, p), key=lambda d: min(d, p - d)):
             pltpu.make_async_remote_copy(
                 src_ref=out_ref.at[s], dst_ref=out_ref.at[s], send_sem=out_send, recv_sem=out_recv, device_id={"sp": other(d)}, device_id_type=MESH
             ).start()
@@ -120,7 +118,8 @@
     for s in (0, 1):
         fetch_k(s + SLOTS, s).start(priority=1)
 
-    def body(s, _):
+    def body(s, before):
+        who = owner(s - 1)
         kslot, vslot = lax.rem(s, SLOTS), lax.rem(s - 2, SLOTS)
         fetch_v(s - 2, vslot).wait()
         fetch_k(s, kslot).wait()
@@ -141,17 +140,18 @@
             pl.semaphore_wait(barrier, p - 1)
 
             def late(u, _):
-                send_stat(u)
-                send_part(u)
+                who = owner(u)
+                send_stat(u, who)
+                send_part(u, who)
                 return 0
 
             lax.fori_loop(0, OPEN - 2, late, 0)
-            send_stat(OPEN - 2)
+            send_stat(OPEN - 2, ORDER[(OPEN - 2) % p])
 
         @pl.when(s >= OPEN)
         def _():
-            send_stat(s - 1)
-            send_part(s - 2)
+            send_stat(s - 1, who)
+            send_part(s - 2, before)
 
         @pl.when(s == FIRST)
         def _():
@@ -161,19 +161,19 @@
         def _():
             together(s - LAG)
 
-        return 0
-
-    lax.fori_loop(2, n, body, 0)
+        return who
+
+    lax.fori_loop(2, n, body, jnp.int32(ORDER[0]))
     slot = (n - 2) % SLOTS
     fetch_v(n - 2, slot).wait()
-    mix(n - 2, slot)
+    mix(n - 2, slot, 2)
     soften(n - 1)
-    send_stat(n - 1)
-    send_part(n - 2)
+    send_stat(n - 1, ORDER[p - 1])
+    send_part(n - 2, ORDER[p - 2])
     slot = (n - 1) % SLOTS
     fetch_v(n - 1, slot).wait()
-    mix(n - 1, slot)
-    send_part(n - 1)
+    mix(n - 1, slot, 2)
+    send_part(n - 1, ORDER[p - 1])
     @pl.when(owned(1) >= n - LAG)
     def _():
         together(owned(1))

time: 36.1 us -> 35.3 us (0.978)
  Pallas kernels: 35.3 us -> 34.5 us
    pallas_call x1, Pallas kernels: 35.3 us -> 34.5 us  [step(): pl.pallas_call(functools.partial(kernel, n, p, rows, heads, head, kv), ou...]
where the time goes in v3:
time: 35.3 us; the launch traced here: 35.2 us
  Pallas kernels  34.5 us (98%)
  local copies, waits for them, and re-layouts  0.71 us (2%)
    pallas_call x1, Pallas kernels, step(): pl.pallas_call(functools.partial(kernel, n, p, rows, heads, head, kv), ou...  34.5 us

profile of v3, /device:TPU:21, one launch (start us, length us, event | category | flops | bytes accessed | tf_op | source)
XLA Modules:
  0.0 35.2 jit_solution(6145859561129409165)
XLA Ops:
  0.0 34.5 %attend.1 = bf16[32,16,256]{2,1,0:T(8,128)(2,1)S(1)} custom-call(bf16[32,16,256]{2,1,0:T(8,128)(2,1)} %q_hbm.1, bf16[32,2048,256]{2,1,0:T(8,128)(2,1)} %bitcast.2, bf16[32,2048,256]{2,1,0:T(8,128)(2,1)} %bitcast.3), custom_call_target="tpu_custom_call" | custom-call | tf_op jit(solution)/shard_map/attend/pallas_call | solution.py:197
  34.5 0.7 %copy.5 = bf16[32,16,256]{2,1,0:T(8,128)(2,1)} copy(bf16[32,16,256]{2,1,0:T(8,128)(2,1)S(1)} %attend.1) | data formatting | bytes 524288

commit v4 on v3

--- a/solution.py
+++ b/solution.py
@@ -12,7 +12,7 @@
 OPEN = 8
 FIRST = 24
 LAG = 16
-ORDER = (4, 10, 6, 12, 8, 14, 2, 11, 7, 9, 3, 13, 5, 0, 15, 1)
+ORDER = (4, 10, 6, 12, 8, 14, 0, 11, 7, 9, 3, 13, 5, 2, 15, 1)
 
 
 def kernel(n, p, rows, heads, head, kv, q_hbm, k_hbm, v_hbm, out_ref, q_ref, kbuf, vbuf, scores, weights, mine, stat, parts, stats,

time: 35.3 us -> 35.3 us (level)
  no operation moved by 1% of the time
where the time goes in v4:
time: 35.3 us; the launch traced here: 35.2 us
  Pallas kernels  34.5 us (98%)
  local copies, waits for them, and re-layouts  0.71 us (2%)
    pallas_call x1, Pallas kernels, step(): pl.pallas_call(functools.partial(kernel, n, p, rows, heads, head, kv), ou...  34.5 us

profile of v4, /device:TPU:21, one launch (start us, length us, event | category | flops | bytes accessed | tf_op | source)
XLA Modules:
  0.0 35.2 jit_solution(16292694182200910162)
XLA Ops:
  0.0 34.5 %attend.1 = bf16[32,16,256]{2,1,0:T(8,128)(2,1)S(1)} custom-call(bf16[32,16,256]{2,1,0:T(8,128)(2,1)} %q_hbm.1, bf16[32,2048,256]{2,1,0:T(8,128)(2,1)} %bitcast.2, bf16[32,2048,256]{2,1,0:T(8,128)(2,1)} %bitcast.3), custom_call_target="tpu_custom_call" | custom-call | tf_op jit(solution)/shard_map/attend/pallas_call | solution.py:197
  34.5 0.7 %copy.5 = bf16[32,16,256]{2,1,0:T(8,128)(2,1)} copy(bf16[32,16,256]{2,1,0:T(8,128)(2,1)S(1)} %attend.1) | data formatting | bytes 524288
